TPU v7x, 32 devices: a whole 2x2x4 slice. The times are simulated.
32 devices in a mesh: patch: 8 (over z, x), member: 4 (over y, core).
Axes of the slice: x: 2, y: 2, z: 4, core: 2. Of those that a mesh axis runs over, the one named last changes fastest.
Arguments:
- background: bfloat16 [32, 16, 3, 64, 128], P('patch', None, None, 'member'), may hold values from -6 to 6
- patch_blocks: int32 [32], replicated, may hold values from 1 to 16, as said below
- obs_values: float32 [16384], P(('patch', 'member')), may hold values from -12 to 12
- obs_errors: float32 [16384], P(('patch', 'member')), may hold values from 0.5 to 2
- obs_patch: int32 [16384], P('patch'), may hold values from 0 to 3
- obs_position: int32 [16384], P('patch'), may hold values from 0 to 1073741823
Outputs:
- analysis: bfloat16 [32, 16, 3, 64, 128], P('patch', None, None, 'member')
- inflation: float32 [], replicated
Inputs may be any that keep to these rules, and one draw needn't show every extreme that they name: `obs_patch`: index among the 4 patches held by the observation's index of patch. `patch_blocks`: the used blocks of the 4 patches of one index of patch sum to at most 32; some index reaches 32, and some patch uses all 16.
All inputs are finite; a program needn't handle non-finite values.
Results may differ from a plain program's by a relative error of at most 0.0065.
Values may be sent and summed in bfloat16 or wider, within the bound.
A program may use at most 64 MiB of HBM per device.

v0:
```python
import math

import jax
import jax.numpy as jnp
from jax import lax
from jax.sharding import PartitionSpec as P

K = 64
CB = 128
MAXB = 16
NS_STEPS = 4
PD = 4
OBS_DEV = 2048


neighbour_weight = 0.5


def extended(array, sides, width):
    for axis, dim in sides:
        count, length = (lax.axis_size(axis), array.shape[dim])
        up = [(i, (i + 1) % count) for i in range(count - 1)]
        down = [(j, i) for i, j in up]
        last = lax.slice_in_dim(array, length - width, length, axis=dim)
        initial = lax.slice_in_dim(array, 0, width, axis=dim)
        before = lax.ppermute(last, axis, up)
        after = lax.ppermute(initial, axis, down)
        array = jnp.concatenate([before, array, after], axis=dim)
    return array


def inverse_root(system):
    precise = lax.Precision.HIGHEST
    identity = jnp.eye(K, dtype=jnp.float32)
    norm_value = jnp.sqrt(jnp.sum(system * system, axis=(1, 2)))
    square_part = system / norm_value[:, None, None]
    inverse_part = jnp.broadcast_to(identity, system.shape)
    for sweep_index in range(NS_STEPS):
        middle = 1.5 * identity - 0.5 * jnp.einsum(
            "pij,pjk->pik", inverse_part, square_part, precision=precise
        )
        square_part = jnp.einsum("pij,pjk->pik", square_part, middle, precision=precise)
        inverse_part = jnp.einsum("pij,pjk->pik", middle, inverse_part, precision=precise)
    return inverse_part / jnp.sqrt(norm_value)[:, None, None]


def per_device(background, patch_blocks, obs_values, obs_errors, obs_patch, obs_position):
    precise = lax.Precision.HIGHEST
    member_count = lax.axis_size("member")
    local_members = K // member_count
    obs_share = OBS_DEV // member_count
    block_share = MAXB // member_count
    member_index = lax.axis_index("member")
    first_patch = lax.axis_index("patch") * PD
    used_blocks = lax.dynamic_slice_in_dim(patch_blocks, first_patch, PD)
    slot_table = jnp.arange(PD, dtype=jnp.int32)
    onehot_all = obs_patch[None, :] == slot_table[:, None]
    obs_counts = jnp.sum(jnp.where(onehot_all, used_blocks[:, None], 0), axis=0)
    cell_index = obs_position % (obs_counts * CB)
    flat_index = obs_patch * (MAXB * CB) + cell_index
    thickness = jnp.transpose(background[:, :, 0], (0, 1, 3, 2)).reshape(
        PD * MAXB * CB, local_members
    )
    sampled_local = thickness[flat_index]
    sampled = lax.all_to_all(sampled_local, "member", split_axis=0, concat_axis=1, tiled=True)
    own_slots = lax.dynamic_slice_in_dim(obs_patch, member_index * obs_share, obs_share)
    values = sampled.astype(jnp.float32)
    obs_mean = jnp.sum(values, axis=1) / K
    spread = values - obs_mean[:, None]
    innovation = obs_values - obs_mean
    variance = jnp.sum(spread * spread, axis=1) / (K - 1)
    misfit_part = jnp.sum(innovation * innovation)
    spread_part = jnp.sum(variance + obs_errors * obs_errors)
    weighted = spread / obs_errors[:, None]
    onehot = (own_slots[None, :] == slot_table[:, None]).astype(jnp.float32)
    masked = onehot[:, :, None] * weighted[None]
    gram_own = jnp.einsum("pjk,jl->pkl", masked, weighted, precision=precise)
    cross_own = jnp.einsum("pjk,j->pk", masked, innovation / obs_errors, precision=precise)
    stacked = jnp.concatenate([gram_own, cross_own[:, None, :]], axis=1)
    summed, misfit_member, spread_member = lax.psum((stacked, misfit_part, spread_part), "member")
    numerator, denominator = lax.psum((misfit_member, spread_member), "patch")
    inflation = numerator / denominator
    rimmed = extended(summed, (("patch", 0),), 1)
    localized = rimmed[1:-1] + neighbour_weight * (rimmed[:-2] + rimmed[2:])
    gram_local = localized[:, :K]
    cross_local = localized[:, K]
    identity = jnp.eye(K, dtype=jnp.float32)
    system = (K - 1) / inflation * identity + gram_local
    root_inverse = inverse_root(system)
    inner_weights = jnp.einsum("pkl,pl->pk", root_inverse, cross_local, precision=precise)
    mean_weights = jnp.einsum("pkl,pl->pk", root_inverse, inner_weights, precision=precise)
    transform = (mean_weights[:, :, None] + math.sqrt(K - 1) * root_inverse).astype(jnp.bfloat16)
    columns = lax.all_to_all(background, "member", split_axis=1, concat_axis=3, tiled=True)
    member_mean = jnp.sum(columns.astype(jnp.float32), axis=3) / K
    anomaly = (columns.astype(jnp.float32) - member_mean[:, :, :, None, :]).astype(jnp.bfloat16)
    combined = jnp.einsum(
        "pbvlc,plk->pbvkc", anomaly, transform, preferred_element_type=jnp.float32
    )
    block_ids = member_index * block_share + jnp.arange(block_share, dtype=jnp.int32)
    in_use = (block_ids[None, :] < used_blocks[:, None])[:, :, None, None, None]
    result = jnp.where(in_use, member_mean[:, :, :, None, :] + combined, 0.0).astype(jnp.bfloat16)
    analysis = lax.all_to_all(result, "member", split_axis=3, concat_axis=1, tiled=True)
    return (analysis, inflation)


def solution(mesh):
    in_specs = (
        P("patch", None, None, "member", None),
        P(),
        P(("patch", "member")),
        P(("patch", "member")),
        P("patch"),
        P("patch"),
    )
    out_specs = (P("patch", None, None, "member", None), P())
    return jax.shard_map(
        per_device, mesh=mesh, in_specs=in_specs, out_specs=out_specs, check_vma=False
    )
```

profile of v0, /device:TPU:0, one launch (start us, length us, event | category | flops | bytes accessed | tf_op | source)
XLA Modules:
  0.0 108.1 jit_solution(4150788410182912282)
XLA Ops:
  7.2 0.0 copy-start.5
  7.2 0.0 copy-start.1
  7.2 0.0 copy-start.3
  7.2 1.0 slice_bitcast_fusion
  8.2 1.0 copy.84
  9.2 0.0 copy-done.5
  9.2 0.1 dynamic_slice.6
  9.3 0.0 copy-done.1
  9.3 0.1 select_reduce_fusion
  9.4 0.1 fusion.30
  9.6 0.0 copy-start
  9.6 6.2 %gather_fusion = bf16[2048,16]{1,0:T(8,128)(2,1)S(1)} fusion(bf16[8192,16]{1,0:T(8,128)(2,1)S(1)} %bitcast.75, s32[2048]{0:T(1024)S(1)} %fusion.30), kind=kCustom, calls=%fused_computation | custom fusion | bytes 139264 | tf_op jit(solution)/shard_map/gather | solution.py:64
  15.8 0.8 copy.85
  16.6 4.3 %all-to-all-start.1 = ((bf16[4,512,16]{1,2,0:T(8,128)(2,1)}), bf16[4,512,16]{1,2,0:T(8,128)(2,1)S(1)}, u32[]{:S(2)}, u32[]{:S(2)}) async-start(bf16[4,512,16]{1,2,0:T(8,128)(2,1)} %copy.85), calls=%async_computation.1 | async-start | bytes 131072 | tf_op jit(solution)/shard_map/all_to_all | solution.py:65
  20.8 0.1 dynamic_slice.7
  20.9 0.1 broadcast_compare_fusion
  21.0 0.0 copy-start.2
  21.0 0.0 copy-start.4
  21.0 1.0 copy.79
  22.0 2.9 %all-to-all-done.1 = bf16[4,512,16]{1,2,0:T(8,128)(2,1)S(1)} async-done(((bf16[4,512,16]{1,2,0:T(8,128)(2,1)}), bf16[4,512,16]{1,2,0:T(8,128)(2,1)S(1)}, u32[]{:S(2)}, u32[]{:S(2)}) %all-to-all-start.1) | async-done | bytes 65568 | tf_op jit(solution)/shard_map/all_to_all | solution.py:65
  25.0 3.5 %all-to-all-start = ((bf16[4,16,3,16,128]{4,3,2,0,1:T(8,128)(2,1)}), bf16[4,16,3,16,128]{4,3,2,0,1:T(8,128)(2,1)S(1)}, u32[]{:S(2)}, u32[]{:S(2)}) async-start(bf16[4,16,3,16,128]{4,3,2,0,1:T(8,128)(2,1)} %copy.79), calls=%async_computation | async-start | bytes 1572864 | tf_op jit(solution)/shard_map/all_to_all | solution.py:93
  28.5 0.0 all-reduce.4.cloned.1.call-start
  28.6 0.0 copy-done.2
  28.6 0.7 multiply_reduce_fusion.2
  29.3 0.9 fusion.7
  30.2 0.5 convolution_bitcast_fusion
  30.7 0.8 pad_maximum_fusion.2
  31.5 0.0 all-reduce.4.cloned.1.call-update
  31.5 0.1 copy.82
  31.6 0.1 copy.83
  31.7 10.3 %all-reduce.1 = (f32[]{:T(128)}, f32[]{:T(128)}) all-reduce(f32[]{:T(128)} %get-tuple-element.10, f32[]{:T(128)} %get-tuple-element.8), channel_id=1, replica_groups=mesh['patch'=8,'member'=4] {'member'}, use_global_device_ids=true, to_apply=%region_6.7 | all-reduce | flops 2 | bytes 16 | tf_op jit(solution)/shard_map/psum | solution.py:80
  42.0 22.8 %all-reduce = (f32[]{:T(128)}, f32[]{:T(128)}) all-reduce(f32[]{:T(128)} %get-tuple-element.4, f32[]{:T(128)} %get-tuple-element.5), channel_id=1, replica_groups=mesh['patch'=8,'member'=4] {'patch'}, use_global_device_ids=true, to_apply=%region_7.8 | all-reduce | flops 2 | bytes 16 | tf_op jit(solution)/shard_map/psum | solution.py:81
  66.1 0.0 all-reduce.4.cloned.1.call-done
  66.2 0.8 fusion.36
  66.9 2.8 %collective-permute-start = (f32[1,65,64]{1,2,0:T(8,128)S(1)}, f32[1,65,64]{1,2,0:T(8,128)S(1)}, u32[]{:S(2)}, u32[]{:S(2)}) collective-permute-start(f32[1,65,64]{1,2,0:T(8,128)S(1)} %get-tuple-element.6), channel_id=1, source_target_pairs={{0,4},{4,8},{8,12},{12,16},{16,20},{20,24},{24,28},{1,5},{5,9},{9,... | collective-permute-start | bytes 49928 | tf_op jit(solution)/shard_map/ppermute | solution.py:26
  69.7 1.3 %collective-permute-start.1 = (f32[1,65,64]{1,2,0:T(8,128)S(1)}, f32[1,65,64]{1,2,0:T(8,128)S(1)}, u32[]{:S(2)}, u32[]{:S(2)}) collective-permute-start(f32[1,65,64]{1,2,0:T(8,128)S(1)} %get-tuple-element.7), channel_id=1, source_target_pairs={{4,0},{8,4},{12,8},{16,12},{20,16},{24,20},{28,24},{5,1},{9,5},{13... | collective-permute-start | bytes 49928 | tf_op jit(solution)/shard_map/ppermute | solution.py:27
  71.1 0.3 collective-permute-done
  71.3 4.2 %collective-permute-done.1 = f32[1,65,64]{1,2,0:T(8,128)S(1)} collective-permute-done((f32[1,65,64]{1,2,0:T(8,128)S(1)}, f32[1,65,64]{1,2,0:T(8,128)S(1)}, u32[]{:S(2)}, u32[]{:S(2)}) %collective-permute-start.1) | collective-permute-done | bytes 16672 | tf_op jit(solution)/shard_map/ppermute | solution.py:27
  75.6 1.1 %fusion.15 = f32[4,65,64]{1,2,0:T(8,128)S(1)} fusion(f32[4,65,64]{1,2,0:T(8,128)} %all-reduce.4.cloned.1.call-done, f32[1,65,64]{1,2,0:T(8,128)S(1)} %collective-permute-done.1, f32[1,65,64]{1,2,0:T(8,128)S(1)} %collective-permute-done), kind=kLoop, calls=%fused_computation.30 | loop fusion | flops 83200 | bytes 166400 | tf_op jit(solution)/shard_map/add | solution.py:84
  76.6 0.1 multiply_reduce_fusion
  76.8 0.4 fusion.5
  77.2 0.5 fusion.33
  77.7 0.3 fusion.23
  77.9 0.3 fusion.4
  78.2 0.3 fusion.38
  78.5 0.3 fusion.37
  78.7 0.3 fusion.3
  79.0 0.3 fusion.40
  79.3 0.3 fusion.39
  79.5 0.3 fusion.2
  79.8 0.3 convolution_divide_fusion
  80.0 0.2 slice_reduce_fusion
  80.2 0.3 convolution_bitcast_fusion.1
  80.5 0.3 fusion.41
  80.9 0.0 all-to-all-done
  80.9 0.4 convert_reduce_fusion
  81.3 0.2 convert_element_type.61
  81.5 0.2 copy.89
  81.7 0.2 fusion
  81.9 0.5 fusion.1
  82.4 1.5 %copy.92 = bf16[4,4,3,64,128]{4,1,2,0,3:T(4,128)(2,1)} copy(bf16[4,4,3,64,128]{4,3,2,1,0:T(8,128)(2,1)S(1)} %fusion.1) | data formatting | bytes 1572864 | tf_op jit(solution)/shard_map/convert_element_type | solution.py:101
  83.9 3.5 %all-to-all-start.2 = ((bf16[4,4,3,64,128]{4,1,2,0,3:T(4,128)(2,1)}), bf16[4,4,3,64,128]{4,1,2,0,3:T(4,128)(2,1)S(1)}, u32[]{:S(2)}, u32[]{:S(2)}) async-start(bf16[4,4,3,64,128]{4,1,2,0,3:T(4,128)(2,1)} %copy.92), calls=%async_computation.2 | async-start | bytes 1572864 | tf_op jit(solution)/shard_map/all_to_all | solution.py:102
  88.7 10.3 %all-to-all-done.2 = bf16[4,4,3,64,128]{4,1,2,0,3:T(4,128)(2,1)S(1)} async-done(((bf16[4,4,3,64,128]{4,1,2,0,3:T(4,128)(2,1)}), bf16[4,4,3,64,128]{4,1,2,0,3:T(4,128)(2,1)S(1)}, u32[]{:S(2)}, u32[]{:S(2)}) %all-to-all-start.2) | async-done | bytes 786464 | tf_op jit(solution)/shard_map/all_to_all | solution.py:102
  99.0 1.1 %copy.93 = bf16[4,4,4,3,16,128]{5,4,3,2,1,0:T(8,128)(2,1)} copy(bf16[4,4,4,3,16,128]{5,2,3,0,4,1:T(4,128)(2,1)S(1)} %bitcast.77) | data formatting | bytes 1572864 | tf_op jit(solution)/shard_map/all_to_all | solution.py:102
  (16 shorter events, 0.2 us)
Async XLA Ops:
  7.2 2.1 %copy-start.5 = (s32[32]{0:T(128)S(1)}, s32[32]{0:T(128)}, u32[]{:S(2)}) copy-start(s32[32]{0:T(128)} %param.7) | copy-start | bytes 388
  7.2 2.1 %copy-start.1 = (s32[2048]{0:T(1024)S(1)}, s32[2048]{0:T(1024)}, u32[]{:S(2)}) copy-start(s32[2048]{0:T(1024)} %param.10) | copy-start | bytes 24580
  7.2 2.2 %copy-start.3 = (s32[2048]{0:T(1024)S(1)}, s32[2048]{0:T(1024)}, u32[]{:S(2)}) copy-start(s32[2048]{0:T(1024)} %param.11) | copy-start | bytes 24580
  9.6 11.4 %copy-start = (bf16[4,16,3,16,128]{4,3,2,1,0:T(8,128)(2,1)S(1)}, bf16[4,16,3,16,128]{4,3,2,1,0:T(8,128)(2,1)}, u32[]{:S(2)}) copy-start(bf16[4,16,3,16,128]{4,3,2,1,0:T(8,128)(2,1)} %param.6) | copy-start | bytes 2359300
  16.6 8.4 %all-to-all-start.1 = ((bf16[4,512,16]{1,2,0:T(8,128)(2,1)}), bf16[4,512,16]{1,2,0:T(8,128)(2,1)S(1)}, u32[]{:S(2)}, u32[]{:S(2)}) async-start(bf16[4,512,16]{1,2,0:T(8,128)(2,1)} %copy.85), calls=%async_computation.1 | async-start | bytes 131072 | tf_op jit(solution)/shard_map/all_to_all | solution.py:65
  21.0 7.6 %copy-start.2 = (f32[512]{0:T(512)S(1)}, f32[512]{0:T(512)}, u32[]{:S(2)}) copy-start(f32[512]{0:T(512)} %param.9) | copy-start | bytes 6148
  21.0 7.6 %copy-start.4 = (f32[512]{0:T(512)S(1)}, f32[512]{0:T(512)}, u32[]{:S(2)}) copy-start(f32[512]{0:T(512)} %param.8) | copy-start | bytes 6148
  25.0 55.9 %all-to-all-start = ((bf16[4,16,3,16,128]{4,3,2,0,1:T(8,128)(2,1)}), bf16[4,16,3,16,128]{4,3,2,0,1:T(8,128)(2,1)S(1)}, u32[]{:S(2)}, u32[]{:S(2)}) async-start(bf16[4,16,3,16,128]{4,3,2,0,1:T(8,128)(2,1)} %copy.79), calls=%async_computation | async-start | bytes 1572864 | tf_op jit(solution)/shard_map/all_to_all | solution.py:93
  28.5 37.7 %all-reduce.4.cloned.1.call-start = ((), (), s32[]{:S(2)}) async-start(), calls=%async_computation.3 | async-start | bytes 262144 | tf_op jit(solution)/shard_map/psum | solution.py:80
  66.9 4.4 %collective-permute-start = (f32[1,65,64]{1,2,0:T(8,128)S(1)}, f32[1,65,64]{1,2,0:T(8,128)S(1)}, u32[]{:S(2)}, u32[]{:S(2)}) collective-permute-start(f32[1,65,64]{1,2,0:T(8,128)S(1)} %get-tuple-element.6), channel_id=1, source_target_pairs={{0,4},{4,8},{8,12},{12,16},{16,20},{20,24},{24,28},{1,5},{5,9},{9,... | collective-permute-start | bytes 49928 | tf_op jit(solution)/shard_map/ppermute | solution.py:26
  69.7 5.8 %collective-permute-start.1 = (f32[1,65,64]{1,2,0:T(8,128)S(1)}, f32[1,65,64]{1,2,0:T(8,128)S(1)}, u32[]{:S(2)}, u32[]{:S(2)}) collective-permute-start(f32[1,65,64]{1,2,0:T(8,128)S(1)} %get-tuple-element.7), channel_id=1, source_target_pairs={{4,0},{8,4},{12,8},{16,12},{20,16},{24,20},{28,24},{5,1},{9,5},{13... | collective-permute-start | bytes 49928 | tf_op jit(solution)/shard_map/ppermute | solution.py:27
  83.9 15.1 %all-to-all-start.2 = ((bf16[4,4,3,64,128]{4,1,2,0,3:T(4,128)(2,1)}), bf16[4,4,3,64,128]{4,1,2,0,3:T(4,128)(2,1)S(1)}, u32[]{:S(2)}, u32[]{:S(2)}) async-start(bf16[4,4,3,64,128]{4,1,2,0,3:T(4,128)(2,1)} %copy.92), calls=%async_computation.2 | async-start | bytes 1572864 | tf_op jit(solution)/shard_map/all_to_all | solution.py:102
Sparse Core Ops, SparseCore 0:
  31.6 33.9 all-reduce.3
where the time goes:
time: 109 us; the launch traced here: 108 us
  blocking collectives  33.1 us (30%)
  between operations  18.1 us (17%)
  waiting for transfers between devices  17.7 us (16%)
  starting transfers between devices  15.4 us (14%)
  local copies, waits for them, and re-layouts  14.1 us (13%)
  matrix products  5.75 us (5%)
  other arithmetic  3.89 us (4%)
    psum x1, blocking collectives, per_device(): numerator, denominator = lax.psum((misfit_member, spread_member), 'patch')  22.8 us
    psum x1, blocking collectives, per_device(): lax.psum((stacked, misfit_part, spread_part), 'member')  10.3 us
    all_to_all x1, waiting for transfers between devices, per_device(): lax.all_to_all(result, 'member', split_axis=3, concat_axis=1, tiled=True)  10.3 us
    gather x1, local copies, waits for them, and re-layouts, per_device(): sampled_local = thickness[flat_index]  6.19 us
    all_to_all x1, starting transfers between devices, per_device(): lax.all_to_all(sampled_local, 'member', split_axis=0, concat_axis=1, tile...  4.26 us
    ppermute x1, waiting for transfers between devices, extended(): after = lax.ppermute(initial, axis, down)  4.23 us
    all_to_all x1, starting transfers between devices, per_device(): lax.all_to_all(background, 'member', split_axis=1, concat_axis=3, tiled=T...  3.49 us
    all_to_all x1, starting transfers between devices, per_device(): lax.all_to_all(result, 'member', split_axis=3, concat_axis=1, tiled=True)  3.49 us
  transfers between devices with their start and end apart: 6, of which 4 were waited for; matrix products, arithmetic and copies ran while one was open for 10% of the time, Pallas kernels for 0%

commit v1 on v0

v1 whole, which is shorter than its diff:
```python
import functools
import math

import jax
import jax.numpy as jnp
from jax import lax
from jax.experimental import pallas as pl
from jax.experimental.pallas import tpu as pltpu
from jax.sharding import PartitionSpec as P

K = 64
DEV_BLOCKS = 32
NS_STEPS = 4
neighbour_weight = 0.5
T_CHUNKS = 4
V_CHUNKS = 4
F32 = jnp.float32
BF16 = jnp.bfloat16


def split2(a):
    hi = a.astype(BF16)
    return hi, (a - hi.astype(F32)).astype(BF16)


def split3(a):
    hi = a.astype(BF16).astype(F32)
    rest = a - hi
    mid = rest.astype(BF16).astype(F32)
    return hi, mid, rest - mid


def dot_nn(a, b):
    return lax.dot_general(a, b, (((1,), (0,)), ((), ())), preferred_element_type=F32)


def dot_nt(a, b):
    return lax.dot_general(a, b, (((1,), (1,)), ((), ())), preferred_element_type=F32)


def product(a, b):
    n = a[0].shape[0]
    both = dot_nn(jnp.concatenate(a, axis=0), b[0])
    return both[:n] + both[n:] + dot_nn(a[0], b[1])


def total(a):
    return jnp.sum(jnp.sum(a, axis=0, keepdims=True), axis=1, keepdims=True)


def kernel(
    n_patch,
    n_member,
    used_ref,
    obs_ref,
    slot_patch_ref,
    position_ref,
    background_ref,
    out_ref,
    inflation_ref,
    own,
    tbuf,
    vbuf,
    obuf,
    wtab,
    mtab,
    ubuf,
    edge_send,
    edge_recv,
    sums,
    grams,
    roots,
    weights,
    defect,
    res,
    own_sem,
    t_send,
    t_recv,
    v_send,
    v_recv,
    o_send,
    o_recv,
    e_send,
    e_recv,
    s_send,
    s_recv,
):
    pd, maxb, nv, local, cb = own.shape
    me = lax.axis_index("member")
    pi = lax.axis_index("patch")
    near = me + 1 - 2 * (me % 2)
    far = (me + n_member // 2) % n_member
    cross = far + 1 - 2 * (far % 2)

    barrier = pltpu.get_barrier_semaphore()
    for peer in (near, far, cross):
        pl.semaphore_signal(
            barrier, inc=1, device_id={"member": peer}, device_id_type=pl.DeviceIdType.MESH
        )

    def greet(i, carry):
        peer = (pi + i) % n_patch
        pl.semaphore_signal(
            barrier, inc=1, device_id={"patch": peer}, device_id_type=pl.DeviceIdType.MESH
        )
        return carry

    lax.fori_loop(1, n_patch, greet, 0)
    load = pltpu.make_async_copy(background_ref, own, own_sem)
    load.start()

    used = [used_ref[pi * pd + p] for p in range(pd)]
    start = [jnp.int32(0)]
    for p in range(pd - 1):
        start.append(start[-1] + used[p])

    def patch_of(s):
        p = jnp.int32(0)
        first = jnp.int32(0)
        for q in range(1, pd):
            inside = s >= start[q]
            p = jnp.where(inside, q, p)
            first = jnp.where(inside, start[q], first)
        return p, jnp.minimum(s - first, maxb - 1)

    slot_patch = slot_patch_ref[...]
    position = position_ref[...]
    blocks = jnp.zeros_like(position)
    offset = jnp.zeros_like(position)
    for p in range(pd):
        blocks = jnp.where(slot_patch == p, used[p], blocks)
        offset = jnp.where(slot_patch == p, start[p], offset)
    lane = position & (cb - 1)
    quotient = position // cb
    blocks_f = blocks.astype(F32)
    rest = quotient - blocks * jnp.floor(quotient.astype(F32) / blocks_f).astype(jnp.int32)
    for _ in range(2):
        rest = jnp.where(rest < 0, rest + blocks, rest)
    for _ in range(2):
        rest = jnp.where(rest >= blocks, rest - blocks, rest)
    slot = offset + rest

    load.wait()
    per = DEV_BLOCKS // T_CHUNKS
    for s in range(DEV_BLOCKS):
        p, b = patch_of(s)
        x = own[p, b]
        tbuf[me, s] = x[0]
        vbuf[me, s] = x[1:]
    obuf[me] = obs_ref[...]

    pl.semaphore_wait(barrier, 3 + n_patch - 1)

    def remote(src, dst, send, recv, **where):
        return pltpu.make_async_remote_copy(
            src_ref=src,
            dst_ref=dst,
            send_sem=send,
            recv_sem=recv,
            device_id=where,
            device_id_type=pl.DeviceIdType.MESH,
        )

    def obs_copy(i, peer, holder):
        return remote(obs_ref, obuf.at[holder], o_send.at[i], o_recv.at[i], member=peer)

    def t_copy(route, c, peer, holder):
        part = tbuf.at[holder, pl.ds(c * per, per)]
        return remote(part, part, t_send.at[route, c], t_recv.at[route, c], member=peer)

    vper = DEV_BLOCKS // V_CHUNKS

    def v_copy(route, c, peer, holder):
        part = vbuf.at[holder, pl.ds(c * vper, vper)]
        return remote(part, part, v_send.at[route, c], v_recv.at[route, c], member=peer)

    for i, peer in enumerate((near, far, cross)):
        obs_copy(i, peer, me).start()
    for c in range(T_CHUNKS):
        t_copy(1, c, far, me).start()
    for c in range(T_CHUNKS):
        t_copy(0, c, near, me).start()
    for c in range(V_CHUNKS):
        v_copy(1, c, far, me).start()
    for c in range(V_CHUNKS):
        v_copy(0, c, near, me).start()

    for i, holder in enumerate((near, far, cross)):
        obs_copy(i, holder, holder).wait_recv()

    rows = DEV_BLOCKS
    n_obs_rows = position.shape[0]
    half = obs_ref.shape[0] // 2
    values = jnp.concatenate([obuf[m, :half] for m in range(n_member)], axis=0)
    errors = jnp.concatenate([obuf[m, half:] for m in range(n_member)], axis=0)
    inverse = 1.0 / (errors * errors)
    parts = [*split3(inverse), *split3(values * inverse), *split3(values), jnp.ones_like(values)]
    slot_rows = lax.broadcasted_iota(jnp.int32, (rows, cb), 0)
    lane_rows = lax.broadcasted_iota(jnp.int32, (cb, cb), 0)
    acc = jnp.zeros((len(parts) * rows, cb), F32)
    for r in range(0, n_obs_rows, 2):
        left, right = [], []
        for q in (r, r + 1):
            hit = slot_rows == slot[q : q + 1]
            left.append(
                jnp.concatenate(
                    [jnp.where(hit, part[q : q + 1], 0.0) for part in parts], axis=0
                ).astype(BF16)
            )
            right.append(jnp.where(lane_rows == lane[q : q + 1], 1.0, 0.0).astype(BF16))
        acc = acc + dot_nt(jnp.concatenate(left, axis=1), jnp.concatenate(right, axis=1))
    tables = [acc[i * rows : (i + 1) * rows] for i in range(len(parts))]
    weight = tables[0] + tables[1] + tables[2]
    pull = tables[3] + tables[4] + tables[5]
    number = tables[9]
    centre = (tables[6] + tables[7] + tables[8]) / jnp.maximum(number, 1.0)
    scale = jnp.sqrt(weight)
    inverse_scale = jnp.where(weight > 0.0, 1.0 / jnp.maximum(scale, 1e-6), 0.0)
    wtab[0] = scale
    wtab[1] = pull * inverse_scale
    centre_parts = jnp.concatenate(split3(centre), axis=0).astype(BF16)
    apart = jnp.zeros((1, cb), F32)
    for q in range(n_obs_rows):
        onehot = jnp.where(lane_rows == lane[q : q + 1], 1.0, 0.0).astype(BF16)
        found = dot_nn(centre_parts, onehot)
        found = found[:rows] + found[rows : 2 * rows] + found[2 * rows :]
        found = jnp.sum(
            jnp.where(slot_rows == slot[q : q + 1], found, 0.0), axis=0, keepdims=True
        )
        apart = apart + (values[q : q + 1] - found) ** 2
    apart = jnp.sum(apart, axis=1, keepdims=True)
    error_sum = total(errors * errors)

    part_row = lax.broadcasted_iota(jnp.int32, (16, cb), 0)

    def centre_chunk(c, carry):
        t_copy(1, c, far, far).wait_recv()
        t_copy(2, c, near, far).start()
        t_copy(0, c, near, near).wait_recv()
        t_copy(2, c, near, cross).wait_recv()
        for i in range(per):
            s = c * per + i
            x = jnp.concatenate([tbuf[m, s] for m in range(n_member)], axis=0).astype(F32)
            mean = jnp.sum(x, axis=0, keepdims=True) / K
            a = x - mean
            mtab[0, pl.ds(s, 1)] = mean
            mtab[1, pl.ds(s, 1)] = jnp.sum(a * a, axis=0, keepdims=True)
            row = wtab[0, pl.ds(s, 1)]
            hi, lo = split2(a * row)
            ubuf[s, :K] = hi
            ubuf[s, K : 2 * K] = lo
            v1, v2, v3 = split3(wtab[1, pl.ds(s, 1)] - mean * row)
            v = jnp.where(
                part_row == 0,
                v1,
                jnp.where(part_row == 1, v2, jnp.where(part_row == 2, v3, 0.0)),
            )
            ubuf[s, 2 * K :] = v.astype(BF16)
        return carry

    lax.fori_loop(0, T_CHUNKS, centre_chunk, 0)
    means = mtab[0]
    misfit = apart + total(number * (centre - means) ** 2)
    spread = error_sum + total(number * mtab[1]) / (K - 1)
    sum_rows = lax.broadcasted_iota(jnp.int32, (8, cb), 0)
    sums[pi] = jnp.where(sum_rows == 0, misfit, spread)

    def sum_copy(slot_index, peer):
        return remote(
            sums.at[slot_index],
            sums.at[slot_index],
            s_send.at[peer],
            s_recv.at[slot_index],
            patch=peer,
        )

    def send_sum(i, carry):
        sum_copy(pi, (pi + i) % n_patch).start()
        return carry

    lax.fori_loop(1, n_patch, send_sum, 0)

    def gram_of(p):
        acc = jnp.zeros((2 * K + 16, 2 * K), F32)
        for b in range(0, maxb, 2):
            pair = []
            for q in (b, b + 1):
                u = ubuf[jnp.minimum(start[p] + q, DEV_BLOCKS - 1)]
                pair.append(jnp.where(q < used[p], u, jnp.zeros_like(u)))
            pair = jnp.concatenate(pair, axis=1)
            acc = acc + dot_nt(pair, pair[: 2 * K])
        g = acc[:K] + acc[K : 2 * K]
        c = jnp.broadcast_to(jnp.sum(acc[2 * K :], axis=0, keepdims=True), (8, 2 * K))
        full = jnp.concatenate([g, c], axis=0)
        return full + pltpu.roll(full, K, 1)

    def edge_copy(i, peer):
        return remote(edge_send.at[i], edge_recv.at[i], e_send.at[i], e_recv.at[i], patch=peer)

    up = (pi + 1) % n_patch
    down = (pi + n_patch - 1) % n_patch
    gram = [None] * pd
    gram[pd - 1] = gram_of(pd - 1)
    edge_send[0] = gram[pd - 1]
    gram[0] = gram_of(0)
    edge_send[1] = gram[0]

    @pl.when(pi < n_patch - 1)
    def _():
        edge_copy(0, up).start()

    @pl.when(pi > 0)
    def _():
        edge_copy(1, down).start()

    for p in range(1, pd - 1):
        gram[p] = gram_of(p)
    for p in range(pd):
        grams[p] = gram[p]

    def relay(c, carry):
        v_copy(1, c, far, far).wait_recv()
        v_copy(2, c, near, far).start()
        return carry

    lax.fori_loop(0, V_CHUNKS, relay, 0)

    @pl.when(pi > 0)
    def _():
        edge_copy(0, up).wait_recv()

    @pl.when(pi == 0)
    def _():
        edge_recv[0] = jnp.zeros(edge_recv.shape[1:], F32)

    @pl.when(pi < n_patch - 1)
    def _():
        edge_copy(1, down).wait_recv()

    @pl.when(pi == n_patch - 1)
    def _():
        edge_recv[1] = jnp.zeros(edge_recv.shape[1:], F32)

    def recv_sum(i, carry):
        peer = (pi + i) % n_patch
        sum_copy(peer, peer).wait_recv()
        return carry

    lax.fori_loop(1, n_patch, recv_sum, 0)
    both = jnp.sum(sums[...], axis=0)
    inflation = both[0:1] / both[1:2]
    inflation_ref[...] = jnp.broadcast_to(inflation, inflation_ref.shape)

    eye = jnp.where(
        lax.broadcasted_iota(jnp.int32, (K, K), 0) == lax.broadcasted_iota(jnp.int32, (K, K), 1),
        1.0,
        0.0,
    )
    field = [edge_recv[0]] + [grams[p] for p in range(pd)] + [edge_recv[1]]
    ridge = (K - 1) / inflation[:, :K]
    square, norm, drive = [], [], []
    for p in range(pd):
        local_field = field[p + 1] + neighbour_weight * (field[p] + field[p + 2])
        system = local_field[:K, :K] + ridge * eye
        drive.append(local_field[K : K + 1, :K])
        size = jnp.sqrt(total(system * system))
        norm.append(size)
        square.append(system / size)
    middle = [1.5 * eye - 0.5 * a for a in square]
    inverse_part = middle
    m_parts = [split2(a) for a in middle]
    z_parts = m_parts
    s_parts = [split2(a) for a in square]
    for sweep in range(1, NS_STEPS):
        square = [product(a, b) for a, b in zip(s_parts, m_parts)]
        s_parts = [split2(a) for a in square]
        middle = [1.5 * eye - 0.5 * product(a, b) for a, b in zip(z_parts, s_parts)]
        m_parts = [split2(a) for a in middle]
        inverse_part = [product(a, b) for a, b in zip(m_parts, z_parts)]
        z_parts = [split2(a) for a in inverse_part]
    for p in range(pd):
        root = inverse_part[p] / jnp.sqrt(norm[p])
        inner = jnp.sum(root * drive[p], axis=1, keepdims=True)
        mean_weights = jnp.sum(root * inner, axis=0, keepdims=True)
        roots[p] = mean_weights + math.sqrt(K - 1) * root
        mine = roots[p, pl.ds(me * local, local)].astype(BF16)
        weights[p, :local] = mine
        weights[p, local:] = jnp.ones((16, K), BF16)
        short = (1.0 - jnp.sum(mine.astype(F32), axis=1, keepdims=True)) / K
        defect[p] = jnp.broadcast_to(short, (local, cb))

    def finish_chunk(c, carry):
        v_copy(0, c, near, near).wait_recv()
        v_copy(2, c, near, cross).wait_recv()
        for i in range(vper):
            s = c * vper + i
            p, _ = patch_of(s)
            w = weights[p]
            d = defect[p]
            thick = jnp.concatenate([tbuf[m, s] for m in range(n_member)], axis=0)
            speeds = [
                jnp.concatenate([vbuf[m, s, v] for m in range(n_member)], axis=0)
                for v in range(nv - 1)
            ]
            got = dot_nn(w, jnp.concatenate([thick] + speeds, axis=1))
            for v in range(nv):
                g = got[:, v * cb : (v + 1) * cb]
                res[s, v] = (g[:local] + g[local : local + 1] * d).astype(BF16)
        return carry

    lax.fori_loop(0, V_CHUNKS, finish_chunk, 0)

    for p in range(pd):
        for b in range(maxb):
            r = res[jnp.minimum(start[p] + b, DEV_BLOCKS - 1)]
            out_ref[p, b] = jnp.where(b < used[p], r, jnp.zeros_like(r))

    for i, peer in enumerate((near, far, cross)):
        obs_copy(i, peer, me).wait_send()
    for c in range(T_CHUNKS):
        t_copy(0, c, near, me).wait_send()
        t_copy(1, c, far, me).wait_send()
        t_copy(2, c, near, far).wait_send()
    for c in range(V_CHUNKS):
        v_copy(0, c, near, me).wait_send()
        v_copy(1, c, far, me).wait_send()
        v_copy(2, c, near, far).wait_send()

    @pl.when(pi < n_patch - 1)
    def _():
        edge_copy(0, up).wait_send()

    @pl.when(pi > 0)
    def _():
        edge_copy(1, down).wait_send()

    def sum_left(i, carry):
        sum_copy(pi, (pi + i) % n_patch).wait_send()
        return carry

    lax.fori_loop(1, n_patch, sum_left, 0)


def solution(mesh):
    n_patch, n_member = mesh.shape["patch"], mesh.shape["member"]

    def per_device(background, patch_blocks, obs_values, obs_errors, obs_patch, obs_position):
        pd, maxb, nv, local, cb = background.shape
        obs = jnp.concatenate([obs_values.reshape(-1, cb), obs_errors.reshape(-1, cb)], axis=0)
        vmem = pl.BlockSpec(memory_space=pltpu.VMEM)
        dma = pltpu.SemaphoreType.DMA
        analysis, inflation = pl.pallas_call(
            functools.partial(kernel, n_patch, n_member),
            out_shape=(
                jax.ShapeDtypeStruct(background.shape, BF16),
                jax.ShapeDtypeStruct((8, cb), F32),
            ),
            in_specs=[
                pl.BlockSpec(memory_space=pltpu.SMEM),
                vmem,
                vmem,
                vmem,
                pl.BlockSpec(memory_space=pl.ANY),
            ],
            out_specs=(vmem, vmem),
            scratch_shapes=[
                pltpu.VMEM(background.shape, BF16),
                pltpu.VMEM((n_member, DEV_BLOCKS, local, cb), BF16),
                pltpu.VMEM((n_member, DEV_BLOCKS, nv - 1, local, cb), BF16),
                pltpu.VMEM((n_member, *obs.shape), F32),
                pltpu.VMEM((2, DEV_BLOCKS, cb), F32),
                pltpu.VMEM((2, DEV_BLOCKS, cb), F32),
                pltpu.VMEM((DEV_BLOCKS, 2 * K + 16, cb), BF16),
                pltpu.VMEM((2, K + 8, 2 * K), F32),
                pltpu.VMEM((2, K + 8, 2 * K), F32),
                pltpu.VMEM((n_patch, 8, cb), F32),
                pltpu.VMEM((pd, K + 8, 2 * K), F32),
                pltpu.VMEM((pd, K, K), F32),
                pltpu.VMEM((pd, local + 16, K), BF16),
                pltpu.VMEM((pd, local, cb), F32),
                pltpu.VMEM((DEV_BLOCKS, nv, local, cb), BF16),
                dma,
                dma((3, T_CHUNKS)),
                dma((3, T_CHUNKS)),
                dma((3, V_CHUNKS)),
                dma((3, V_CHUNKS)),
                dma((3,)),
                dma((3,)),
                dma((2,)),
                dma((2,)),
                dma((n_patch,)),
                dma((n_patch,)),
            ],
            compiler_params=pltpu.CompilerParams(collective_id=0, has_side_effects=True),
        )(
            patch_blocks,
            obs,
            obs_patch.reshape(-1, cb),
            obs_position.reshape(-1, cb),
            background,
        )
        return analysis, inflation[0, 0]

    in_specs = (
        P("patch", None, None, "member", None),
        P(),
        P(("patch", "member")),
        P(("patch", "member")),
        P("patch"),
        P("patch"),
    )
    out_specs = (P("patch", None, None, "member", None), P())
    return jax.shard_map(
        per_device, mesh=mesh, in_specs=in_specs, out_specs=out_specs, check_vma=False
    )
```

time: 109 us -> 28.9 us (0.27)
  blocking collectives: 33.1 us -> 0 us
  Pallas kernels: 0 us -> 23.4 us
  waiting for transfers between devices: 17.7 us -> 0 us
  between operations: 18.1 us -> 0.66 us
  starting transfers between devices: 15.4 us -> 0 us
  local copies, waits for them, and re-layouts: 14.1 us -> 3.96 us
  matrix products: 5.75 us -> 0 us
  other arithmetic: 3.89 us -> 0.6 us
    psum x2 -> x0, blocking collectives: 33.1 us -> none  [the longest x1 22.8 us: per_device(): numerator, denominator = lax.psum((misfit_member, spread_member), 'patch')]
    pallas_call x0 -> x1, Pallas kernels: none -> 23.4 us  [per_device(): pl.pallas_call(functools.partial(kernel, n_patch, n_member), out_shape=(j...]
    all_to_all x3 -> x0, waiting for transfers between devices: 13.2 us -> none  [the longest x1 10.3 us: per_device(): lax.all_to_all(result, 'member', split_axis=3, concat_axis=1, tiled=True)]
    all_to_all x3 -> x0, starting transfers between devices: 11.3 us -> none  [the longest x1 4.26 us: per_device(): lax.all_to_all(sampled_local, 'member', split_axis=0, concat_axis=1, tile...]
    gather x1 -> x0, local copies, waits for them, and re-layouts: 6.19 us -> none  [per_device(): sampled_local = thickness[flat_index]]
    dot_general x16 -> x0, matrix products: 5.75 us -> none  [the longest x4 1.19 us: inverse_root(): jnp.einsum('pij,pjk->pik', inverse_part, square_part, precision=precise)]
    ppermute x2 -> x0, waiting for transfers between devices: 4.49 us -> none  [the longest x1 4.23 us: extended(): after = lax.ppermute(initial, axis, down)]
    ppermute x2 -> x0, starting transfers between devices: 4.08 us -> none  [the longest x1 2.79 us: extended(): before = lax.ppermute(last, axis, up)]
  transfers between devices with their start and end apart: 6 -> 0, of which waited for: 4 -> 0; matrix products, arithmetic and copies ran while one was open for 10% -> 0% of each run, Pallas kernels for 0% -> 0%
where the time goes in v1:
time: 28.9 us; the launch traced here: 28.6 us
  Pallas kernels  23.4 us (81%)
  local copies, waits for them, and re-layouts  3.96 us (14%)
  between operations  0.66 us (2%)
  other arithmetic  0.6 us (2%)
    pallas_call x1, Pallas kernels, per_device(): pl.pallas_call(functools.partial(kernel, n_patch, n_member), out_shape=(j...  23.4 us
    unnamed x5, local copies, waits for them, and re-layouts  2.77 us
    slice x1, local copies, waits for them, and re-layouts, per_device(): return (analysis, inflation[0, 0])  1.19 us
    concatenate x1, other arithmetic, per_device(): jnp.concatenate([obs_values.reshape(-1, cb), obs_errors.reshape(-1, cb)],...  0.6 us

profile of v1, /device:TPU:0, one launch (start us, length us, event | category | flops | bytes accessed | tf_op | source)
XLA Modules:
  0.0 28.6 jit_solution(14674653812615877302)
XLA Ops:
  0.6 0.0 copy-start.1
  0.6 0.0 copy-start
  0.6 0.7 %copy-done.1 = f32[512]{0:T(512)S(1)} copy-done((f32[512]{0:T(512)S(1)}, f32[512]{0:T(512)}, u32[]{:S(2)}) %copy-start.1) | copy-done | bytes 2072
  1.3 0.0 copy-done
  1.3 0.6 %pad_maximum_fusion.obs_ref = f32[8,128]{1,0:T(8,128)} fusion(f32[4,128]{1,0:T(4,128)S(1)} %bitcast.7, f32[4,128]{1,0:T(4,128)S(1)} %bitcast.8), kind=kLoop, calls=%fused_computation | loop fusion | flops 1024 | bytes 8192 | tf_op jit(solution)/shard_map/concatenate | solution.py:449
  1.9 23.4 %shard_map.77 = (bf16[4,16,3,16,128]{4,3,2,1,0:T(8,128)(2,1)}, f32[8,128]{1,0:T(8,128)}) custom-call(s32[32]{0:T(128)} %used_ref.1, f32[8,128]{1,0:T(8,128)} %pad_maximum_fusion.obs_ref, s32[16,128]{1,0:T(8,128)} %bitcast.5, s32[16,128]{1,0:T(8,128)} %bitcast.6, bf16[4,16,3,16,128]{4,3,2,1,0:T(8,128)(2,1)} %background_ref.1), custom_call_target="tpu_custom_call" | custom-call | tf_op jit(solution)/shard_map/pallas_call | solution.py:452
  25.3 1.2 %slice.3 = f32[1,1]{1,0:T(1,128)} slice(f32[8,128]{1,0:T(8,128)} %get-tuple-element.5), slice={[0:1], [0:1]} | slice | bytes 8 | tf_op jit(solution)/shard_map/slice | solution.py:502
  26.5 2.1 %copy.9 = bf16[4,16,3,16,128]{4,3,2,1,0:T(8,128)(2,1)} copy(bf16[4,16,3,16,128]{4,3,2,1,0:T(8,128)(2,1)} %get-tuple-element.8) | data formatting | bytes 1572864
Async XLA Ops:
  0.6 0.7 %copy-start.1 = (f32[512]{0:T(512)S(1)}, f32[512]{0:T(512)}, u32[]{:S(2)}) copy-start(f32[512]{0:T(512)} %param.8) | copy-start | bytes 6148
  0.6 0.7 %copy-start = (f32[512]{0:T(512)S(1)}, f32[512]{0:T(512)}, u32[]{:S(2)}) copy-start(f32[512]{0:T(512)} %param.9) | copy-start | bytes 6148

commit v2 on v1

--- a/solution.py
+++ b/solution.py
@@ -52,13 +52,17 @@
     n_patch,
     n_member,
     used_ref,
+    values_ref,
+    errors_ref,
+    slot_patch_hbm,
+    position_hbm,
+    background_ref,
+    res,
+    inflation_ref,
+    own,
     obs_ref,
     slot_patch_ref,
     position_ref,
-    background_ref,
-    out_ref,
-    inflation_ref,
-    own,
     tbuf,
     vbuf,
     obuf,
@@ -72,8 +76,8 @@
     roots,
     weights,
     defect,
-    res,
     own_sem,
+    in_sem,
     t_send,
     t_recv,
     v_send,
@@ -106,6 +110,19 @@
         return carry
 
     lax.fori_loop(1, n_patch, greet, 0)
+    small = [
+        pltpu.make_async_copy(source, target, in_sem.at[i])
+        for i, (source, target) in enumerate(
+            (
+                (values_ref, obs_ref.at[0]),
+                (errors_ref, obs_ref.at[1]),
+                (slot_patch_hbm, slot_patch_ref),
+                (position_hbm, position_ref),
+            )
+        )
+    ]
+    for copy in small:
+        copy.start()
     load = pltpu.make_async_copy(background_ref, own, own_sem)
     load.start()
 
@@ -123,6 +140,8 @@
             first = jnp.where(inside, start[q], first)
         return p, jnp.minimum(s - first, maxb - 1)
 
+    for copy in small:
+        copy.wait()
     slot_patch = slot_patch_ref[...]
     position = position_ref[...]
     blocks = jnp.zeros_like(position)
@@ -190,9 +209,8 @@
 
     rows = DEV_BLOCKS
     n_obs_rows = position.shape[0]
-    half = obs_ref.shape[0] // 2
-    values = jnp.concatenate([obuf[m, :half] for m in range(n_member)], axis=0)
-    errors = jnp.concatenate([obuf[m, half:] for m in range(n_member)], axis=0)
+    values = jnp.concatenate([obuf[m, 0] for m in range(n_member)], axis=0)
+    errors = jnp.concatenate([obuf[m, 1] for m in range(n_member)], axis=0)
     inverse = 1.0 / (errors * errors)
     parts = [*split3(inverse), *split3(values * inverse), *split3(values), jnp.ones_like(values)]
     slot_rows = lax.broadcasted_iota(jnp.int32, (rows, cb), 0)
@@ -233,9 +251,17 @@
 
     part_row = lax.broadcasted_iota(jnp.int32, (16, cb), 0)
 
-    def centre_chunk(c, carry):
+    def forward(c):
         t_copy(1, c, far, far).wait_recv()
         t_copy(2, c, near, far).start()
+
+    forward(0)
+
+    def centre_chunk(c, carry):
+        @pl.when(c + 1 < T_CHUNKS)
+        def _():
+            forward(c + 1)
+
         t_copy(0, c, near, near).wait_recv()
         t_copy(2, c, near, cross).wait_recv()
         for i in range(per):
@@ -349,7 +375,7 @@
     lax.fori_loop(1, n_patch, recv_sum, 0)
     both = jnp.sum(sums[...], axis=0)
     inflation = both[0:1] / both[1:2]
-    inflation_ref[...] = jnp.broadcast_to(inflation, inflation_ref.shape)
+    inflation_ref[0, 0] = jnp.max(inflation)
 
     eye = jnp.where(
         lax.broadcasted_iota(jnp.int32, (K, K), 0) == lax.broadcasted_iota(jnp.int32, (K, K), 1),
@@ -410,11 +436,6 @@
 
     lax.fori_loop(0, V_CHUNKS, finish_chunk, 0)
 
-    for p in range(pd):
-        for b in range(maxb):
-            r = res[jnp.minimum(start[p] + b, DEV_BLOCKS - 1)]
-            out_ref[p, b] = jnp.where(b < used[p], r, jnp.zeros_like(r))
-
     for i, peer in enumerate((near, far, cross)):
         obs_copy(i, peer, me).wait_send()
     for c in range(T_CHUNKS):
@@ -441,33 +462,53 @@
     lax.fori_loop(1, n_patch, sum_left, 0)
 
 
+def expand_kernel(pd, used_ref, inflation_in, res, out_ref, inflation_out):
+    p = pl.program_id(0)
+    first = lax.axis_index("patch") * pd
+    start = jnp.int32(0)
+    for q in range(pd):
+        start = start + jnp.where(q < p, used_ref[first + q], 0)
+    used = used_ref[first + p]
+    for b in range(out_ref.shape[1]):
+        r = res[jnp.minimum(start + b, DEV_BLOCKS - 1)]
+        out_ref[0, b] = jnp.where(b < used, r, jnp.zeros_like(r))
+    inflation_out[0, 0] = inflation_in[0, 0]
+
+
 def solution(mesh):
     n_patch, n_member = mesh.shape["patch"], mesh.shape["member"]
 
     def per_device(background, patch_blocks, obs_values, obs_errors, obs_patch, obs_position):
         pd, maxb, nv, local, cb = background.shape
-        obs = jnp.concatenate([obs_values.reshape(-1, cb), obs_errors.reshape(-1, cb)], axis=0)
+        values, errors = obs_values.reshape(-1, cb), obs_errors.reshape(-1, cb)
+        slot_patch, position = obs_patch.reshape(-1, cb), obs_position.reshape(-1, cb)
         vmem = pl.BlockSpec(memory_space=pltpu.VMEM)
+        smem = pl.BlockSpec(memory_space=pltpu.SMEM)
+        hbm = pl.BlockSpec(memory_space=pl.ANY)
         dma = pltpu.SemaphoreType.DMA
-        analysis, inflation = pl.pallas_call(
+        packed, ratio = pl.pallas_call(
             functools.partial(kernel, n_patch, n_member),
             out_shape=(
-                jax.ShapeDtypeStruct(background.shape, BF16),
-                jax.ShapeDtypeStruct((8, cb), F32),
+                jax.ShapeDtypeStruct((DEV_BLOCKS, nv, local, cb), BF16),
+                jax.ShapeDtypeStruct((1, 1), F32),
             ),
             in_specs=[
-                pl.BlockSpec(memory_space=pltpu.SMEM),
-                vmem,
-                vmem,
-                vmem,
-                pl.BlockSpec(memory_space=pl.ANY),
+                smem,
+                hbm,
+                hbm,
+                hbm,
+                hbm,
+                hbm,
             ],
-            out_specs=(vmem, vmem),
+            out_specs=(vmem, smem),
             scratch_shapes=[
                 pltpu.VMEM(background.shape, BF16),
+                pltpu.VMEM((2, *values.shape), F32),
+                pltpu.VMEM(slot_patch.shape, jnp.int32),
+                pltpu.VMEM(position.shape, jnp.int32),
                 pltpu.VMEM((n_member, DEV_BLOCKS, local, cb), BF16),
                 pltpu.VMEM((n_member, DEV_BLOCKS, nv - 1, local, cb), BF16),
-                pltpu.VMEM((n_member, *obs.shape), F32),
+                pltpu.VMEM((n_member, 2, *values.shape), F32),
                 pltpu.VMEM((2, DEV_BLOCKS, cb), F32),
                 pltpu.VMEM((2, DEV_BLOCKS, cb), F32),
                 pltpu.VMEM((DEV_BLOCKS, 2 * K + 16, cb), BF16),
@@ -478,8 +519,8 @@
                 pltpu.VMEM((pd, K, K), F32),
                 pltpu.VMEM((pd, local + 16, K), BF16),
                 pltpu.VMEM((pd, local, cb), F32),
-                pltpu.VMEM((DEV_BLOCKS, nv, local, cb), BF16),
                 dma,
+                dma((4,)),
                 dma((3, T_CHUNKS)),
                 dma((3, T_CHUNKS)),
                 dma((3, V_CHUNKS)),
@@ -494,12 +535,26 @@
             compiler_params=pltpu.CompilerParams(collective_id=0, has_side_effects=True),
         )(
             patch_blocks,
-            obs,
-            obs_patch.reshape(-1, cb),
-            obs_position.reshape(-1, cb),
+            values,
+            errors,
+            slot_patch,
+            position,
             background,
         )
-        return analysis, inflation[0, 0]
+        analysis, inflation = pl.pallas_call(
+            functools.partial(expand_kernel, pd),
+            grid=(pd,),
+            out_shape=(
+                jax.ShapeDtypeStruct(background.shape, BF16),
+                jax.ShapeDtypeStruct((1, 1), F32),
+            ),
+            in_specs=[smem, smem, vmem],
+            out_specs=(
+                pl.BlockSpec((1, maxb, nv, local, cb), lambda p: (p, 0, 0, 0, 0)),
+                smem,
+            ),
+        )(patch_blocks, ratio, packed)
+        return analysis, inflation.reshape(())
 
     in_specs = (
         P("patch", None, None, "member", None),

time: 28.9 us -> 25.5 us (0.88)
  local copies, waits for them, and re-layouts: 3.96 us -> 0 us
  Pallas kernels: 23.4 us -> 24.6 us
  other arithmetic: 0.6 us -> 0 us
    pallas_call x0 -> x1, Pallas kernels: none -> 3.35 us  [per_device(): pl.pallas_call(functools.partial(expand_kernel, pd), grid=(pd,), out_shap...]
    unnamed x5 -> x0, local copies, waits for them, and re-layouts: 2.77 us -> none
    pallas_call x1, Pallas kernels: 23.4 us -> 21.3 us  [per_device(): pl.pallas_call(functools.partial(kernel, n_patch, n_member), out_shape=(j...]
    slice x1 -> x0, local copies, waits for them, and re-layouts: 1.19 us -> none  [per_device(): return (analysis, inflation[0, 0])]
    concatenate x1 -> x0, other arithmetic: 0.6 us -> none  [per_device(): jnp.concatenate([obs_values.reshape(-1, cb), obs_errors.reshape(-1, cb)],...]
where the time goes in v2:
time: 25.5 us; the launch traced here: 25.3 us
  Pallas kernels  24.6 us (96%)
  between operations  0.64 us (3%)
    pallas_call x1, Pallas kernels, per_device(): pl.pallas_call(functools.partial(kernel, n_patch, n_member), out_shape=(j...  21.3 us
    pallas_call x1, Pallas kernels, per_device(): pl.pallas_call(functools.partial(expand_kernel, pd), grid=(pd,), out_shap...  3.35 us

profile of v2, /device:TPU:0, one launch (start us, length us, event | category | flops | bytes accessed | tf_op | source)
XLA Modules:
  0.0 25.3 jit_solution(4275351778223095915)
XLA Ops:
  0.6 21.3 %shard_map.77 = (bf16[32,3,16,128]{3,2,1,0:T(8,128)(2,1)}, f32[1,1]{1,0:T(1,128)}) custom-call(s32[32]{0:T(128)} %used_ref.3, f32[4,128]{1,0:T(4,128)} %bitcast.7, f32[4,128]{1,0:T(4,128)} %bitcast.8, s32[16,128]{1,0:T(8,128)} %bitcast.5, s32[16,128]{1,0:T(8,128)} %bitcast.6, bf16[4,16,3,16,128]{4,3,2,1,0:T(8,128)(2,1)} %background_ref.1), custom_call_target="tpu_custom_call" | custom-call | tf_op jit(solution)/shard_map/pallas_call | solution.py:489
  21.9 3.4 %shard_map.78 = (bf16[4,16,3,16,128]{4,3,2,1,0:T(8,128)(2,1)}, f32[1,1]{1,0:T(1,128)}) custom-call(s32[32]{0:T(128)} %used_ref.3, f32[1,1]{1,0:T(1,128)} %get-tuple-element.6.inflation_in, bf16[32,3,16,128]{3,2,1,0:T(8,128)(2,1)} %get-tuple-element.7.res), custom_call_target="tpu_custom_call" | custom-call | tf_op jit(solution)/shard_map/pallas_call | solution.py:544

commit v3 on v2

--- a/solution.py
+++ b/solution.py
@@ -13,7 +13,7 @@
 NS_STEPS = 4
 neighbour_weight = 0.5
 T_CHUNKS = 4
-V_CHUNKS = 4
+V_CHUNKS = 2
 F32 = jnp.float32
 BF16 = jnp.bfloat16
 

time: 25.5 us -> 25.1 us (0.984)
  Pallas kernels: 24.6 us -> 24.3 us
    pallas_call x1, Pallas kernels: 21.3 us -> 20.9 us  [per_device(): pl.pallas_call(functools.partial(kernel, n_patch, n_member), out_shape=(j...]
where the time goes in v3:
time: 25.1 us; the launch traced here: 24.9 us
  Pallas kernels  24.3 us (97%)
  between operations  0.64 us (3%)
    pallas_call x1, Pallas kernels, per_device(): pl.pallas_call(functools.partial(kernel, n_patch, n_member), out_shape=(j...  20.9 us
    pallas_call x1, Pallas kernels, per_device(): pl.pallas_call(functools.partial(expand_kernel, pd), grid=(pd,), out_shap...  3.35 us

profile of v3, /device:TPU:0, one launch (start us, length us, event | category | flops | bytes accessed | tf_op | source)
XLA Modules:
  0.0 24.9 jit_solution(12093317702843998939)
XLA Ops:
  0.6 20.9 %shard_map.77 = (bf16[32,3,16,128]{3,2,1,0:T(8,128)(2,1)}, f32[1,1]{1,0:T(1,128)}) custom-call(s32[32]{0:T(128)} %used_ref.3, f32[4,128]{1,0:T(4,128)} %bitcast.7, f32[4,128]{1,0:T(4,128)} %bitcast.8, s32[16,128]{1,0:T(8,128)} %bitcast.5, s32[16,128]{1,0:T(8,128)} %bitcast.6, bf16[4,16,3,16,128]{4,3,2,1,0:T(8,128)(2,1)} %background_ref.1), custom_call_target="tpu_custom_call" | custom-call | tf_op jit(solution)/shard_map/pallas_call | solution.py:489
  21.5 3.4 %shard_map.78 = (bf16[4,16,3,16,128]{4,3,2,1,0:T(8,128)(2,1)}, f32[1,1]{1,0:T(1,128)}) custom-call(s32[32]{0:T(128)} %used_ref.3, f32[1,1]{1,0:T(1,128)} %get-tuple-element.6.inflation_in, bf16[32,3,16,128]{3,2,1,0:T(8,128)(2,1)} %get-tuple-element.7.res), custom_call_target="tpu_custom_call" | custom-call | tf_op jit(solution)/shard_map/pallas_call | solution.py:544
